TPU v7x, 32 devices: a whole 2x2x4 slice. The times are simulated.
32 devices in a mesh: kv: 2 (over x), batch: 16 (over z, y, core).
Axes of the slice: x: 2, y: 2, z: 4, core: 2. Of those that a mesh axis runs over, the one named last changes fastest.
Arguments:
- queries: bfloat16 [64, 32, 128], P(('kv', 'batch')), may hold values from -64 to 64
- prefix_keys: bfloat16 [8192, 8, 128], P('batch', 'kv'), may hold values from -6 to 6
- prefix_values: bfloat16 [8192, 8, 128], P('batch', 'kv'), may hold values from -6 to 6
- suffix_keys: bfloat16 [64, 2048, 8, 128], P('batch', None, 'kv'), may hold values from -6 to 6
- suffix_values: bfloat16 [64, 2048, 8, 128], P('batch', None, 'kv'), may hold values from -6 to 6
- suffix_lengths: int32 [64], P('batch'), may hold values from 512 to 2048, as said below
- slot_sequence: int32 [64], P('batch'), may hold values from 0 to 63, as said below
Outputs:
- attended: bfloat16 [64, 32, 128], P(('kv', 'batch'))
Inputs may be any that keep to these rules, and one draw needn't show every extreme that they name: `suffix_lengths`: some slot holds exactly 2048 live tokens. `slot_sequence`: each sequence's suffix occupies exactly one slot; the 64 / 16 slots of one index of batch hold sequences whose output rows lie on pairwise different indices of batch.
All inputs are finite; a program needn't handle non-finite values.
Results may differ from a plain program's by a relative error of at most 0.007.
Values may be sent and summed in bfloat16 or wider, within the bound.
A program may use at most 64 MiB of HBM per device.

v0:
```python
import jax
import jax.numpy as jnp
from jax import lax
from jax.sharding import PartitionSpec as P

negative_fill = -1e30


def fold_block(state, keys_part, values_part, grouped, scale):
    best, total, accum = state
    scores = (
        jnp.einsum("rkjd,tkd->rkjt", grouped, keys_part, preferred_element_type=jnp.float32) * scale
    )
    new_best = jnp.maximum(best, jnp.max(scores, axis=-1))
    weights = jnp.exp(scores - new_best[..., None])
    total = jnp.sum(weights, axis=-1)
    accum = jnp.einsum(
        "rkjt,tkd->rkjd",
        weights.astype(jnp.bfloat16),
        values_part,
        preferred_element_type=jnp.float32,
    )
    return (new_best, total, accum)


def merge_rows(best, total, accum, row_ids, part_best, part_total, part_acc):
    old_best = best[row_ids]
    new_best = jnp.maximum(old_best, part_best)
    first = jnp.exp(old_best - new_best)
    second = jnp.exp(part_best - new_best)
    best = best.at[row_ids].set(new_best)
    total = total.at[row_ids].set(total[row_ids] * first + part_total * second)
    accum = accum.at[row_ids].set(accum[row_ids] * first[..., None] + part_acc * second[..., None])
    return (best, total, accum)


def shards(
    queries, prefix_keys, prefix_values, suffix_keys, suffix_values, suffix_lengths, slot_sequence
):
    kv_count = lax.axis_size("kv")
    batch_count = lax.axis_size("batch")
    per_device = queries.shape[0]
    head_count = queries.shape[1]
    head_dim = queries.shape[2]
    local_heads = head_count // kv_count
    kv_local = prefix_keys.shape[1]
    group_size = local_heads // kv_local
    scale = head_dim ** (-0.5)
    relayed = lax.all_to_all(queries, "kv", split_axis=1, concat_axis=0, tiled=True)
    gathered = lax.all_gather(relayed, "batch", axis=0, tiled=True)
    batch_total = gathered.shape[0]
    everyone = gathered.reshape(batch_count, kv_count, per_device, local_heads, head_dim)
    everyone = everyone.transpose(1, 0, 2, 3, 4).reshape(batch_total, local_heads, head_dim)
    slots = suffix_keys.shape[0]
    suffix_len = suffix_keys.shape[1]
    slot_queries = jnp.take(everyone, slot_sequence, axis=0).reshape(
        slots, kv_local, group_size, head_dim
    )
    scores = (
        jnp.einsum("skjd,stkd->skjt", slot_queries, suffix_keys, preferred_element_type=jnp.float32)
        * scale
    )
    position = jnp.arange(suffix_len)
    scores = jnp.where(
        position[None, None, None, :] < suffix_lengths[:, None, None, None], scores, negative_fill
    )
    suf_best = jnp.max(scores, axis=-1)
    weights = jnp.exp(scores - suf_best[..., None])
    suf_total = jnp.sum(weights, axis=-1)
    suf_acc = jnp.einsum(
        "skjt,stkd->skjd",
        weights.astype(jnp.bfloat16),
        suffix_values,
        preferred_element_type=jnp.float32,
    )
    grouped_all = everyone.reshape(batch_total, kv_local, group_size, head_dim)
    start_state = (
        jnp.full((batch_total, kv_local, group_size), negative_fill, jnp.float32),
        jnp.zeros((batch_total, kv_local, group_size), jnp.float32),
        jnp.zeros((batch_total, kv_local, group_size, head_dim), jnp.float32),
    )
    best, total, accum = fold_block(start_state, prefix_keys, prefix_values, grouped_all, scale)
    best, total, accum = merge_rows(best, total, accum, slot_sequence, suf_best, suf_total, suf_acc)
    got_acc, got_best, got_total = (
        lax.all_to_all(
            lax.all_to_all(
                accum.reshape(batch_total, 1, local_heads, head_dim),
                "kv",
                split_axis=0,
                concat_axis=2,
                tiled=True,
            ),
            "batch",
            split_axis=0,
            concat_axis=1,
            tiled=True,
        ),
        lax.all_to_all(
            lax.all_to_all(
                best.reshape(batch_total, 1, local_heads),
                "kv",
                split_axis=0,
                concat_axis=2,
                tiled=True,
            ),
            "batch",
            split_axis=0,
            concat_axis=1,
            tiled=True,
        ),
        lax.all_to_all(
            lax.all_to_all(
                total.reshape(batch_total, 1, local_heads),
                "kv",
                split_axis=0,
                concat_axis=2,
                tiled=True,
            ),
            "batch",
            split_axis=0,
            concat_axis=1,
            tiled=True,
        ),
    )
    top = jnp.max(got_best, axis=1)
    factor = jnp.exp(got_best - top[:, None, :])
    denominator = jnp.sum(got_total * factor, axis=1)
    numerator = jnp.sum(got_acc * factor[..., None], axis=1)
    return (numerator / denominator[..., None]).astype(jnp.bfloat16)


def solution(mesh):
    return jax.shard_map(
        shards,
        mesh=mesh,
        in_specs=(
            P(("kv", "batch"), None, None),
            P("batch", "kv", None),
            P("batch", "kv", None),
            P("batch", None, "kv", None),
            P("batch", None, "kv", None),
            P("batch"),
            P("batch"),
        ),
        out_specs=P(("kv", "batch"), None, None),
        check_vma=False,
    )
```

profile of v0, /device:TPU:0, one launch (start us, length us, event | category | flops | bytes accessed | tf_op | source)
XLA Modules:
  0.0 114.2 jit_solution(14936565666871693103)
XLA Ops:
  0.0 1.4 %copy.73 = bf16[2,32,128]{2,0,1:T(2,128)(2,1)} copy(bf16[2,32,128]{2,1,0:T(8,128)(2,1)} %param.7) | data formatting | bytes 32768 | tf_op args[0]
  1.4 4.2 %all-to-all-start = ((bf16[2,32,128]{2,0,1:T(2,128)(2,1)}), bf16[2,32,128]{2,0,1:T(2,128)(2,1)S(1)}, u32[]{:S(2)}, u32[]{:S(2)}) async-start(bf16[2,32,128]{2,0,1:T(2,128)(2,1)} %copy.73), calls=%async_computation | async-start | bytes 32768 | tf_op jit(solution)/shard_map/all_to_all | solution.py:49
  7.0 0.7 iota_compare_fusion
  7.7 1.8 %all-to-all-done = bf16[2,32,128]{2,0,1:T(2,128)(2,1)S(1)} async-done(((bf16[2,32,128]{2,0,1:T(2,128)(2,1)}), bf16[2,32,128]{2,0,1:T(2,128)(2,1)S(1)}, u32[]{:S(2)}, u32[]{:S(2)}) %all-to-all-start) | async-done | bytes 16416 | tf_op jit(solution)/shard_map/all_to_all | solution.py:49
  9.5 22.8 %all_gather.3 = bf16[64,16,128]{2,1,0:T(8,128)(2,1)S(1)} all-gather(bf16[4,16,128]{2,1,0:T(8,128)(2,1)S(1)} %bitcast.81), channel_id=1, replica_groups=mesh['kv'=2,'batch'=16] {'batch'}, dimensions={0}, use_global_device_ids=true | all-gather | bytes 278528 | tf_op jit(solution)/shard_map/all_gather | solution.py:50
  32.6 1.6 %bitcast_reduce_fusion = (f32[64,4,4]{0,2,1:T(4,128)S(1)}, f32[4,512,64,4]{1,2,3,0:T(8,128)S(1)}) fusion(bf16[64,4,4,128]{3,0,2,1:T(8,128)(2,1)S(1)} %bitcast.73, bf16[512,4,128,1]{2,1,0,3:T(4,128)(2,1)} %bitcast.74), kind=kOutput, calls=%fused_computation.14 | convolution fusion | flops 135265280 | bytes 2887680 | tf_op jit(solution)/shard_map/rkjd,tkd->rkjt/dot_general | solution.py:12
  36.8 5.8 %fusion.34 = (f32[4,4,4]{2,1,0:T(4,128)S(1)}, f32[4,4,4,2048]{3,2,1,0:T(4,128)S(1)}) fusion(bf16[4,2048,4,128]{3,2,1,0:T(4,128)(2,1)} %param.10, bf16[4,4,4,128]{3,2,1,0:T(4,128)(2,1)S(1)} %bitcast.95, pred[4]{0:T(512)(128)(4,1)S(1)} %compare_and_fusion, pred[4,2048]{1,0:T(4,128)(4,1)S(1)} %iota_compare_fusion), kind=kOutput, calls=%fused_computation.47 | convolution fusion | flops 33955776 | bytes 8937732 | tf_op jit(solution)/shard_map/skjd,stkd->skjt/dot_general | solution.py:60
  45.5 3.2 %all-to-all-start.5 = ((f32[2,1,512]{2,1,0:T(1,128)}), f32[2,1,512]{2,1,0:T(1,128)S(1)}, u32[]{:S(2)}, u32[]{:S(2)}) async-start(f32[2,1,512]{2,1,0:T(1,128)} %reshape.140), calls=%async_computation.5 | async-start | bytes 8192 | tf_op jit(solution)/shard_map/all_to_all | solution.py:112
  50.8 1.7 %all-to-all-done.5 = f32[2,1,512]{2,1,0:T(1,128)S(1)} async-done(((f32[2,1,512]{2,1,0:T(1,128)}), f32[2,1,512]{2,1,0:T(1,128)S(1)}, u32[]{:S(2)}, u32[]{:S(2)}) %all-to-all-start.5) | async-done | bytes 4128 | tf_op jit(solution)/shard_map/all_to_all | solution.py:112
  52.5 3.2 %all-to-all-start.3 = ((f32[2,1,512]{2,1,0:T(1,128)}), f32[2,1,512]{2,1,0:T(1,128)S(1)}, u32[]{:S(2)}, u32[]{:S(2)}) async-start(f32[2,1,512]{2,1,0:T(1,128)} %reshape.138), calls=%async_computation.3 | async-start | bytes 8192 | tf_op jit(solution)/shard_map/all_to_all | solution.py:99
  56.3 1.1 copy.84
  57.5 1.6 %gather_fusion = f32[4,4,4,128]{3,2,1,0:T(4,128)S(1)} fusion(f32[64,4,4,128]{3,2,1,0:T(4,128)} %copy.84, s32[1024]{0:T(1024)S(1)} %pad_clamp_fusion), kind=kCustom, calls=%fused_computation | custom fusion | bytes 65552 | tf_op jit(solution)/shard_map/gather | solution.py:33
  59.9 0.7 copy.100
  60.6 3.5 %all-to-all-start.6 = ((f32[32,1,32]{2,1,0:T(1,128)}), f32[32,1,32]{2,1,0:T(1,128)S(1)}, u32[]{:S(2)}, u32[]{:S(2)}) async-start(f32[32,1,32]{2,1,0:T(1,128)} %copy.100), calls=%async_computation.6 | async-start | bytes 32768 | tf_op jit(solution)/shard_map/all_to_all | solution.py:111
  64.1 4.7 %fusion.16 = f32[4,4,4,128]{3,2,1,0:T(4,128)S(1)} fusion(bf16[4,2048,4,128]{3,2,1,0:T(4,128)(2,1)} %param.11, f32[4,4,4,2048]{3,2,1,0:T(4,128)S(1)} %get-tuple-element.14, f32[4,4,4]{2,1,0:T(4,128)S(1)} %get-tuple-element.13, f32[4,4,4,128]{3,2,1,0:T(4,128)S(1)} %gather_fusion, f32[4,4,4]{2,1,0:T(4,128)S(1)} %bitcast.97, f32[4,4,4]{2,1,0:T(4,128)S(1)} %bitcast.96), kind=kOutput, calls=%fused_computation.20 | convolution fusion | flops 33841152 | bytes 8979200 | tf_op jit(solution)/shard_map/skjt,stkd->skjd/dot_general | solution.py:70
  68.8 1.9 %scatter_fusion = f32[64,4,4,128]{3,2,1,0:T(4,128)} fusion(f32[64,4,4,128]{3,2,1,0:T(4,128)} %copy.84, s32[4]{0:T(128)S(1)} %compare_select_fusion, f32[4,4,4,128]{3,2,1,0:T(4,128)S(1)} %fusion.16), kind=kCustom, calls=%fused_computation.4 | custom fusion | bytes 98320 | tf_op jit(solution)/shard_map/scatter | solution.py:33
  70.7 3.5 %all-to-all-start.1 = ((f32[64,1,16,128]{3,2,1,0:T(8,128)}), f32[64,1,16,128]{3,2,1,0:T(8,128)S(1)}, u32[]{:S(2)}, u32[]{:S(2)}) async-start(f32[64,1,16,128]{3,2,1,0:T(8,128)} %bitcast.14), calls=%async_computation.1 | async-start | bytes 1048576 | tf_op jit(solution)/shard_map/all_to_all | solution.py:86
  75.7 7.4 %all-to-all-done.1 = f32[64,1,16,128]{3,2,1,0:T(8,128)S(1)} async-done(((f32[64,1,16,128]{3,2,1,0:T(8,128)}), f32[64,1,16,128]{3,2,1,0:T(8,128)S(1)}, u32[]{:S(2)}, u32[]{:S(2)}) %all-to-all-start.1) | async-done | bytes 524320 | tf_op jit(solution)/shard_map/all_to_all | solution.py:86
  83.2 5.8 %all-to-all-start.4 = ((f32[32,1,32]{2,1,0:T(1,128)}), f32[32,1,32]{2,1,0:T(1,128)S(1)}, u32[]{:S(2)}, u32[]{:S(2)}) async-start(f32[32,1,32]{2,1,0:T(1,128)} %copy.93), calls=%async_computation.4 | async-start | bytes 32768 | tf_op jit(solution)/shard_map/all_to_all | solution.py:98
  89.0 0.9 copy.86
  89.8 5.6 %all-to-all-done.4 = f32[32,1,32]{2,1,0:T(1,128)S(1)} async-done(((f32[32,1,32]{2,1,0:T(1,128)}), f32[32,1,32]{2,1,0:T(1,128)S(1)}, u32[]{:S(2)}, u32[]{:S(2)}) %all-to-all-start.4) | async-done | bytes 4128 | tf_op jit(solution)/shard_map/all_to_all | solution.py:98
  95.5 3.6 %all-to-all-start.2 = ((f32[32,1,32,128]{3,2,1,0:T(8,128)}), f32[32,1,32,128]{3,2,1,0:T(8,128)S(1)}, u32[]{:S(2)}, u32[]{:S(2)}) async-start(f32[32,1,32,128]{3,2,1,0:T(8,128)} %bitcast.18), calls=%async_computation.2 | async-start | bytes 1048576 | tf_op jit(solution)/shard_map/all_to_all | solution.py:85
  99.1 14.2 %all-to-all-done.2 = f32[32,1,32,128]{3,2,1,0:T(8,128)S(1)} async-done(((f32[32,1,32,128]{3,2,1,0:T(8,128)}), f32[32,1,32,128]{3,2,1,0:T(8,128)S(1)}, u32[]{:S(2)}, u32[]{:S(2)}) %all-to-all-start.2) | async-done | bytes 524320 | tf_op jit(solution)/shard_map/all_to_all | solution.py:85
  113.5 0.7 divide_convert_fusion
  (44 shorter events, 12.3 us)
Async XLA Ops:
  0.0 55.7 %copy-start = (bf16[512,4,128]{2,1,0:T(4,128)(2,1)S(1)}, bf16[512,4,128]{2,1,0:T(4,128)(2,1)}, u32[]{:S(2)}) copy-start(bf16[512,4,128]{2,1,0:T(4,128)(2,1)} %param.9) | copy-start | bytes 1572868
  1.4 8.1 %all-to-all-start = ((bf16[2,32,128]{2,0,1:T(2,128)(2,1)}), bf16[2,32,128]{2,0,1:T(2,128)(2,1)S(1)}, u32[]{:S(2)}, u32[]{:S(2)}) async-start(bf16[2,32,128]{2,0,1:T(2,128)(2,1)} %copy.73), calls=%async_computation | async-start | bytes 32768 | tf_op jit(solution)/shard_map/all_to_all | solution.py:49
  45.5 7.0 %all-to-all-start.5 = ((f32[2,1,512]{2,1,0:T(1,128)}), f32[2,1,512]{2,1,0:T(1,128)S(1)}, u32[]{:S(2)}, u32[]{:S(2)}) async-start(f32[2,1,512]{2,1,0:T(1,128)} %reshape.140), calls=%async_computation.5 | async-start | bytes 8192 | tf_op jit(solution)/shard_map/all_to_all | solution.py:112
  52.5 8.0 %all-to-all-start.3 = ((f32[2,1,512]{2,1,0:T(1,128)}), f32[2,1,512]{2,1,0:T(1,128)S(1)}, u32[]{:S(2)}, u32[]{:S(2)}) async-start(f32[2,1,512]{2,1,0:T(1,128)} %reshape.138), calls=%async_computation.3 | async-start | bytes 8192 | tf_op jit(solution)/shard_map/all_to_all | solution.py:99
  60.6 10.2 %all-to-all-start.6 = ((f32[32,1,32]{2,1,0:T(1,128)}), f32[32,1,32]{2,1,0:T(1,128)S(1)}, u32[]{:S(2)}, u32[]{:S(2)}) async-start(f32[32,1,32]{2,1,0:T(1,128)} %copy.100), calls=%async_computation.6 | async-start | bytes 32768 | tf_op jit(solution)/shard_map/all_to_all | solution.py:111
  70.7 12.4 %all-to-all-start.1 = ((f32[64,1,16,128]{3,2,1,0:T(8,128)}), f32[64,1,16,128]{3,2,1,0:T(8,128)S(1)}, u32[]{:S(2)}, u32[]{:S(2)}) async-start(f32[64,1,16,128]{3,2,1,0:T(8,128)} %bitcast.14), calls=%async_computation.1 | async-start | bytes 1048576 | tf_op jit(solution)/shard_map/all_to_all | solution.py:86
  83.2 12.3 %all-to-all-start.4 = ((f32[32,1,32]{2,1,0:T(1,128)}), f32[32,1,32]{2,1,0:T(1,128)S(1)}, u32[]{:S(2)}, u32[]{:S(2)}) async-start(f32[32,1,32]{2,1,0:T(1,128)} %copy.93), calls=%async_computation.4 | async-start | bytes 32768 | tf_op jit(solution)/shard_map/all_to_all | solution.py:98
  95.5 17.8 %all-to-all-start.2 = ((f32[32,1,32,128]{3,2,1,0:T(8,128)}), f32[32,1,32,128]{3,2,1,0:T(8,128)S(1)}, u32[]{:S(2)}, u32[]{:S(2)}) async-start(f32[32,1,32,128]{3,2,1,0:T(8,128)} %bitcast.18), calls=%async_computation.2 | async-start | bytes 1048576 | tf_op jit(solution)/shard_map/all_to_all | solution.py:85
where the time goes:
time: 115 us; the launch traced here: 114 us
  waiting for transfers between devices  30.7 us (27%)
  starting transfers between devices  27 us (23%)
  blocking collectives  22.8 us (20%)
  local copies, waits for them, and re-layouts  14.4 us (13%)
  matrix products  12.6 us (11%)
  other arithmetic  6.31 us (5%)
    all_gather x1, blocking collectives, shards(): gathered = lax.all_gather(relayed, 'batch', axis=0, tiled=True)  22.8 us
    all_to_all x1, waiting for transfers between devices, shards(): lax.all_to_all(lax.all_to_all(accum.reshape(batch_total, 1, local_heads,...  14.2 us
    all_to_all x1, waiting for transfers between devices, shards(): lax.all_to_all(accum.reshape(batch_total, 1, local_heads, head_dim), 'kv'...  7.45 us
    all_to_all x1, starting transfers between devices, shards(): lax.all_to_all(lax.all_to_all(best.reshape(batch_total, 1, local_heads),...  5.81 us
    dot_general x1, matrix products, shards(): jnp.einsum('skjd,stkd->skjt', slot_queries, suffix_keys, preferred_elemen...  5.77 us
    all_to_all x1, waiting for transfers between devices, shards(): lax.all_to_all(lax.all_to_all(best.reshape(batch_total, 1, local_heads),...  5.64 us
    dot_general x1, matrix products, shards(): jnp.einsum('skjt,stkd->skjd', weights.astype(jnp.bfloat16), suffix_values...  4.73 us
    all_to_all x1, starting transfers between devices, shards(): lax.all_to_all(queries, 'kv', split_axis=1, concat_axis=0, tiled=True)  4.23 us
  transfers between devices with their start and end apart: 7, of which 5 were waited for; matrix products, arithmetic and copies ran while one was open for 16% of the time, Pallas kernels for 0%

commit v1 on v0

--- a/solution.py
+++ b/solution.py
@@ -47,7 +47,14 @@
     group_size = local_heads // kv_local
     scale = head_dim ** (-0.5)
     relayed = lax.all_to_all(queries, "kv", split_axis=1, concat_axis=0, tiled=True)
-    gathered = lax.all_gather(relayed, "batch", axis=0, tiled=True)
+    ring = [relayed]
+    for hop in range(15):
+        ring.append(lax.ppermute(ring[-1], "batch", [(dev, (dev + 1) % 16) for dev in range(16)]))
+    gathered = jnp.roll(
+        jnp.concatenate(ring[::-1], axis=0),
+        (lax.axis_index("batch") + 1) * ring[0].shape[0],
+        axis=0,
+    )
     batch_total = gathered.shape[0]
     everyone = gathered.reshape(batch_count, kv_count, per_device, local_heads, head_dim)
     everyone = everyone.transpose(1, 0, 2, 3, 4).reshape(batch_total, local_heads, head_dim)

time: 115 us -> 180 us (1.57)
  waiting for transfers between devices: 30.7 us -> 115 us
  blocking collectives: 22.8 us -> 7.89 us
  starting transfers between devices: 27 us -> 22.9 us
    ppermute x0 -> x15, waiting for transfers between devices: none -> 85.8 us  [shards(): lax.ppermute(ring[-1], 'batch', [(dev, (dev + 1) % 16) for dev in range(1...]
    all_gather x1 -> x0, blocking collectives: 22.8 us -> none  [shards(): gathered = lax.all_gather(relayed, 'batch', axis=0, tiled=True)]
    all_to_all x0 -> x1, blocking collectives: none -> 7.89 us  [shards(): lax.all_to_all(queries, 'kv', split_axis=1, concat_axis=0, tiled=True)]
    all_to_all x1 -> x0, starting transfers between devices: 4.23 us -> none  [shards(): lax.all_to_all(queries, 'kv', split_axis=1, concat_axis=0, tiled=True)]
  transfers between devices with their start and end apart: 7 -> 21, of which waited for: 5 -> 19; matrix products, arithmetic and copies ran while one was open for 16% -> 11% of each run, Pallas kernels for 0% -> 0%
where the time goes in v1:
time: 180 us; the launch traced here: 179 us
  waiting for transfers between devices  115 us (64%)
  starting transfers between devices  22.9 us (13%)
  local copies, waits for them, and re-layouts  14.2 us (8%)
  matrix products  12.6 us (7%)
  blocking collectives  7.89 us (4%)
  other arithmetic  6.32 us (4%)
    ppermute x15, waiting for transfers between devices, shards(): lax.ppermute(ring[-1], 'batch', [(dev, (dev + 1) % 16) for dev in range(1...  85.8 us
    all_to_all x1, waiting for transfers between devices, shards(): lax.all_to_all(lax.all_to_all(accum.reshape(batch_total, 1, local_heads,...  14.2 us
    all_to_all x1, blocking collectives, shards(): lax.all_to_all(queries, 'kv', split_axis=1, concat_axis=0, tiled=True)  7.89 us
    all_to_all x1, waiting for transfers between devices, shards(): lax.all_to_all(accum.reshape(batch_total, 1, local_heads, head_dim), 'kv'...  7.45 us
    all_to_all x1, starting transfers between devices, shards(): lax.all_to_all(lax.all_to_all(best.reshape(batch_total, 1, local_heads),...  5.81 us
    dot_general x1, matrix products, shards(): jnp.einsum('skjd,stkd->skjt', slot_queries, suffix_keys, preferred_elemen...  5.78 us
    all_to_all x1, waiting for transfers between devices, shards(): lax.all_to_all(lax.all_to_all(best.reshape(batch_total, 1, local_heads),...  5.65 us
    dot_general x1, matrix products, shards(): jnp.einsum('skjt,stkd->skjd', weights.astype(jnp.bfloat16), suffix_values...  4.66 us
  transfers between devices with their start and end apart: 21, of which 19 were waited for; matrix products, arithmetic and copies ran while one was open for 11% of the time, Pallas kernels for 0%

profile of v1, /device:TPU:0, one launch (start us, length us, event | category | flops | bytes accessed | tf_op | source)
XLA Modules:
  0.0 178.9 jit_solution(13730221630633711597)
XLA Ops:
  0.8 7.9 %all_to_all.126 = bf16[2,32,128]{2,0,1:T(2,128)(2,1)S(1)} all-to-all(bf16[2,32,128]{2,0,1:T(2,128)(2,1)S(1)} %copy.73), channel_id=1, replica_groups=mesh['kv'=2,'batch'=16] {'kv'}, dimensions={1} | all-to-all | bytes 32768 | tf_op jit(solution)/shard_map/all_to_all | solution.py:49
  8.8 5.8 %collective-permute-done = bf16[4,16,128]{2,1,0:T(8,128)(2,1)S(1)} collective-permute-done((bf16[4,16,128]{2,1,0:T(8,128)(2,1)S(1)}, bf16[4,16,128]{2,1,0:T(8,128)(2,1)S(1)}, u32[]{:S(2)}, u32[]{:S(2)}) %collective-permute-start) | collective-permute-done | bytes 16416 | tf_op jit(solution)/shard_map/ppermute | solution.py:52
  14.6 5.9 %collective-permute-done.1 = bf16[4,16,128]{2,1,0:T(8,128)(2,1)S(1)} collective-permute-done((bf16[4,16,128]{2,1,0:T(8,128)(2,1)S(1)}, bf16[4,16,128]{2,1,0:T(8,128)(2,1)S(1)}, u32[]{:S(2)}, u32[]{:S(2)}) %collective-permute-start.1) | collective-permute-done | bytes 16416 | tf_op jit(solution)/shard_map/ppermute | solution.py:52
  20.5 5.9 %collective-permute-done.2 = bf16[4,16,128]{2,1,0:T(8,128)(2,1)S(1)} collective-permute-done((bf16[4,16,128]{2,1,0:T(8,128)(2,1)S(1)}, bf16[4,16,128]{2,1,0:T(8,128)(2,1)S(1)}, u32[]{:S(2)}, u32[]{:S(2)}) %collective-permute-start.2) | collective-permute-done | bytes 16416 | tf_op jit(solution)/shard_map/ppermute | solution.py:52
  26.3 5.9 %collective-permute-done.3 = bf16[4,16,128]{2,1,0:T(8,128)(2,1)S(1)} collective-permute-done((bf16[4,16,128]{2,1,0:T(8,128)(2,1)S(1)}, bf16[4,16,128]{2,1,0:T(8,128)(2,1)S(1)}, u32[]{:S(2)}, u32[]{:S(2)}) %collective-permute-start.3) | collective-permute-done | bytes 16416 | tf_op jit(solution)/shard_map/ppermute | solution.py:52
  32.2 5.9 %collective-permute-done.4 = bf16[4,16,128]{2,1,0:T(8,128)(2,1)S(1)} collective-permute-done((bf16[4,16,128]{2,1,0:T(8,128)(2,1)S(1)}, bf16[4,16,128]{2,1,0:T(8,128)(2,1)S(1)}, u32[]{:S(2)}, u32[]{:S(2)}) %collective-permute-start.4) | collective-permute-done | bytes 16416 | tf_op jit(solution)/shard_map/ppermute | solution.py:52
  38.1 5.9 %collective-permute-done.5 = bf16[4,16,128]{2,1,0:T(8,128)(2,1)S(1)} collective-permute-done((bf16[4,16,128]{2,1,0:T(8,128)(2,1)S(1)}, bf16[4,16,128]{2,1,0:T(8,128)(2,1)S(1)}, u32[]{:S(2)}, u32[]{:S(2)}) %collective-permute-start.5) | collective-permute-done | bytes 16416 | tf_op jit(solution)/shard_map/ppermute | solution.py:52
  43.9 5.9 %collective-permute-done.6 = bf16[4,16,128]{2,1,0:T(8,128)(2,1)S(1)} collective-permute-done((bf16[4,16,128]{2,1,0:T(8,128)(2,1)S(1)}, bf16[4,16,128]{2,1,0:T(8,128)(2,1)S(1)}, u32[]{:S(2)}, u32[]{:S(2)}) %collective-permute-start.6) | collective-permute-done | bytes 16416 | tf_op jit(solution)/shard_map/ppermute | solution.py:52
  49.8 5.9 %collective-permute-done.7 = bf16[4,16,128]{2,1,0:T(8,128)(2,1)S(1)} collective-permute-done((bf16[4,16,128]{2,1,0:T(8,128)(2,1)S(1)}, bf16[4,16,128]{2,1,0:T(8,128)(2,1)S(1)}, u32[]{:S(2)}, u32[]{:S(2)}) %collective-permute-start.7) | collective-permute-done | bytes 16416 | tf_op jit(solution)/shard_map/ppermute | solution.py:52
  55.6 5.9 %collective-permute-done.8 = bf16[4,16,128]{2,1,0:T(8,128)(2,1)S(1)} collective-permute-done((bf16[4,16,128]{2,1,0:T(8,128)(2,1)S(1)}, bf16[4,16,128]{2,1,0:T(8,128)(2,1)S(1)}, u32[]{:S(2)}, u32[]{:S(2)}) %collective-permute-start.8) | collective-permute-done | bytes 16416 | tf_op jit(solution)/shard_map/ppermute | solution.py:52
  61.5 5.9 %collective-permute-done.9 = bf16[4,16,128]{2,1,0:T(8,128)(2,1)S(1)} collective-permute-done((bf16[4,16,128]{2,1,0:T(8,128)(2,1)S(1)}, bf16[4,16,128]{2,1,0:T(8,128)(2,1)S(1)}, u32[]{:S(2)}, u32[]{:S(2)}) %collective-permute-start.9) | collective-permute-done | bytes 16416 | tf_op jit(solution)/shard_map/ppermute | solution.py:52
  67.4 5.9 %collective-permute-done.10 = bf16[4,16,128]{2,1,0:T(8,128)(2,1)S(1)} collective-permute-done((bf16[4,16,128]{2,1,0:T(8,128)(2,1)S(1)}, bf16[4,16,128]{2,1,0:T(8,128)(2,1)S(1)}, u32[]{:S(2)}, u32[]{:S(2)}) %collective-permute-start.10) | collective-permute-done | bytes 16416 | tf_op jit(solution)/shard_map/ppermute | solution.py:52
  74.0 5.1 %collective-permute-done.11 = bf16[4,16,128]{2,1,0:T(8,128)(2,1)S(1)} collective-permute-done((bf16[4,16,128]{2,1,0:T(8,128)(2,1)S(1)}, bf16[4,16,128]{2,1,0:T(8,128)(2,1)S(1)}, u32[]{:S(2)}, u32[]{:S(2)}) %collective-permute-start.11) | collective-permute-done | bytes 16416 | tf_op jit(solution)/shard_map/ppermute | solution.py:52
  79.8 5.2 %collective-permute-done.12 = bf16[4,16,128]{2,1,0:T(8,128)(2,1)S(1)} collective-permute-done((bf16[4,16,128]{2,1,0:T(8,128)(2,1)S(1)}, bf16[4,16,128]{2,1,0:T(8,128)(2,1)S(1)}, u32[]{:S(2)}, u32[]{:S(2)}) %collective-permute-start.12) | collective-permute-done | bytes 16416 | tf_op jit(solution)/shard_map/ppermute | solution.py:52
  85.6 5.2 %collective-permute-done.13 = bf16[4,16,128]{2,1,0:T(8,128)(2,1)S(1)} collective-permute-done((bf16[4,16,128]{2,1,0:T(8,128)(2,1)S(1)}, bf16[4,16,128]{2,1,0:T(8,128)(2,1)S(1)}, u32[]{:S(2)}, u32[]{:S(2)}) %collective-permute-start.13) | collective-permute-done | bytes 16416 | tf_op jit(solution)/shard_map/ppermute | solution.py:52
  90.8 5.8 %collective-permute-done.14 = bf16[4,16,128]{2,1,0:T(8,128)(2,1)S(1)} collective-permute-done((bf16[4,16,128]{2,1,0:T(8,128)(2,1)S(1)}, bf16[4,16,128]{2,1,0:T(8,128)(2,1)S(1)}, u32[]{:S(2)}, u32[]{:S(2)}) %collective-permute-start.14) | collective-permute-done | bytes 16416 | tf_op jit(solution)/shard_map/ppermute | solution.py:52
  100.5 5.8 %fusion.34 = (f32[4,4,4]{2,1,0:T(4,128)S(1)}, f32[4,4,4,2048]{3,2,1,0:T(4,128)S(1)}) fusion(bf16[4,2048,4,128]{3,2,1,0:T(4,128)(2,1)} %param.10, bf16[4,4,4,128]{3,2,1,0:T(4,128)(2,1)S(1)} %bitcast.97, pred[4]{0:T(512)(128)(4,1)S(1)} %compare_and_fusion, pred[4,2048]{1,0:T(4,128)(4,1)S(1)} %iota_compare_fusion), kind=kOutput, calls=%fused_computation.80 | convolution fusion | flops 33955776 | bytes 8937732 | tf_op jit(solution)/shard_map/skjd,stkd->skjt/dot_general | solution.py:67
  125.3 3.5 %all-to-all-start.6 = ((f32[32,1,32]{2,1,0:T(1,128)}), f32[32,1,32]{2,1,0:T(1,128)S(1)}, u32[]{:S(2)}, u32[]{:S(2)}) async-start(f32[32,1,32]{2,1,0:T(1,128)} %copy.100), calls=%async_computation.6 | async-start | bytes 32768 | tf_op jit(solution)/shard_map/all_to_all | solution.py:118
  128.9 4.7 %fusion.16 = f32[4,4,4,128]{3,2,1,0:T(4,128)S(1)} fusion(bf16[4,2048,4,128]{3,2,1,0:T(4,128)(2,1)} %param.11, f32[4,4,4,2048]{3,2,1,0:T(4,128)S(1)} %get-tuple-element.14, f32[4,4,4]{2,1,0:T(4,128)S(1)} %get-tuple-element.13, f32[4,4,4,128]{3,2,1,0:T(4,128)S(1)} %gather_fusion, f32[4,4,4]{2,1,0:T(4,128)S(1)} %bitcast.99, f32[4,4,4]{2,1,0:T(4,128)S(1)} %bitcast.98), kind=kOutput, calls=%fused_computation.20 | convolution fusion | flops 33841152 | bytes 8979200 | tf_op jit(solution)/shard_map/skjt,stkd->skjd/dot_general | solution.py:77
  140.4 7.5 %all-to-all-done.1 = f32[64,1,16,128]{3,2,1,0:T(8,128)S(1)} async-done(((f32[64,1,16,128]{3,2,1,0:T(8,128)}), f32[64,1,16,128]{3,2,1,0:T(8,128)S(1)}, u32[]{:S(2)}, u32[]{:S(2)}) %all-to-all-start.1) | async-done | bytes 524320 | tf_op jit(solution)/shard_map/all_to_all | solution.py:93
  147.9 5.8 %all-to-all-start.4 = ((f32[32,1,32]{2,1,0:T(1,128)}), f32[32,1,32]{2,1,0:T(1,128)S(1)}, u32[]{:S(2)}, u32[]{:S(2)}) async-start(f32[32,1,32]{2,1,0:T(1,128)} %copy.93), calls=%async_computation.4 | async-start | bytes 32768 | tf_op jit(solution)/shard_map/all_to_all | solution.py:105
  154.5 5.7 %all-to-all-done.4 = f32[32,1,32]{2,1,0:T(1,128)S(1)} async-done(((f32[32,1,32]{2,1,0:T(1,128)}), f32[32,1,32]{2,1,0:T(1,128)S(1)}, u32[]{:S(2)}, u32[]{:S(2)}) %all-to-all-start.4) | async-done | bytes 4128 | tf_op jit(solution)/shard_map/all_to_all | solution.py:105
  160.2 3.6 %all-to-all-start.2 = ((f32[32,1,32,128]{3,2,1,0:T(8,128)}), f32[32,1,32,128]{3,2,1,0:T(8,128)S(1)}, u32[]{:S(2)}, u32[]{:S(2)}) async-start(f32[32,1,32,128]{3,2,1,0:T(8,128)} %bitcast.18), calls=%async_computation.2 | async-start | bytes 1048576 | tf_op jit(solution)/shard_map/all_to_all | solution.py:92
  163.8 14.2 %all-to-all-done.2 = f32[32,1,32,128]{3,2,1,0:T(8,128)S(1)} async-done(((f32[32,1,32,128]{3,2,1,0:T(8,128)}), f32[32,1,32,128]{3,2,1,0:T(8,128)S(1)}, u32[]{:S(2)}, u32[]{:S(2)}) %all-to-all-start.2) | async-done | bytes 524320 | tf_op jit(solution)/shard_map/all_to_all | solution.py:92
  (105 shorter events, 34.3 us)
Async XLA Ops:
  0.0 97.4 %copy-start = (bf16[512,4,128]{2,1,0:T(4,128)(2,1)S(1)}, bf16[512,4,128]{2,1,0:T(4,128)(2,1)}, u32[]{:S(2)}) copy-start(bf16[512,4,128]{2,1,0:T(4,128)(2,1)} %param.8) | copy-start | bytes 1572868
  8.7 5.9 %collective-permute-start = (bf16[4,16,128]{2,1,0:T(8,128)(2,1)S(1)}, bf16[4,16,128]{2,1,0:T(8,128)(2,1)S(1)}, u32[]{:S(2)}, u32[]{:S(2)}) collective-permute-start(bf16[4,16,128]{2,1,0:T(8,128)(2,1)S(1)} %bitcast.78), channel_id=1, source_target_pairs={{0,1},{1,2},{2,3},{3,4},{4,5},{5,6},{6,7},{7,8},{8,9},{9,10},{10,1... | collective-permute-start | bytes 49160 | tf_op jit(solution)/shard_map/ppermute | solution.py:52
  14.6 5.9 %collective-permute-start.1 = (bf16[4,16,128]{2,1,0:T(8,128)(2,1)S(1)}, bf16[4,16,128]{2,1,0:T(8,128)(2,1)S(1)}, u32[]{:S(2)}, u32[]{:S(2)}) collective-permute-start(bf16[4,16,128]{2,1,0:T(8,128)(2,1)S(1)} %collective-permute-done), channel_id=1, source_target_pairs={{0,1},{1,2},{2,3},{3,4},{4,5},{5,6},{6,7},{7,8},{8,9},{9,10},{10,1... | collective-permute-start | bytes 49160 | tf_op jit(solution)/shard_map/ppermute | solution.py:52
  20.5 5.9 %collective-permute-start.2 = (bf16[4,16,128]{2,1,0:T(8,128)(2,1)S(1)}, bf16[4,16,128]{2,1,0:T(8,128)(2,1)S(1)}, u32[]{:S(2)}, u32[]{:S(2)}) collective-permute-start(bf16[4,16,128]{2,1,0:T(8,128)(2,1)S(1)} %collective-permute-done.1), channel_id=1, source_target_pairs={{0,1},{1,2},{2,3},{3,4},{4,5},{5,6},{6,7},{7,8},{8,9},{9,10},{10,1... | collective-permute-start | bytes 49160 | tf_op jit(solution)/shard_map/ppermute | solution.py:52
  26.3 5.9 %collective-permute-start.3 = (bf16[4,16,128]{2,1,0:T(8,128)(2,1)S(1)}, bf16[4,16,128]{2,1,0:T(8,128)(2,1)S(1)}, u32[]{:S(2)}, u32[]{:S(2)}) collective-permute-start(bf16[4,16,128]{2,1,0:T(8,128)(2,1)S(1)} %collective-permute-done.2), channel_id=1, source_target_pairs={{0,1},{1,2},{2,3},{3,4},{4,5},{5,6},{6,7},{7,8},{8,9},{9,10},{10,1... | collective-permute-start | bytes 49160 | tf_op jit(solution)/shard_map/ppermute | solution.py:52
  32.2 5.9 %collective-permute-start.4 = (bf16[4,16,128]{2,1,0:T(8,128)(2,1)S(1)}, bf16[4,16,128]{2,1,0:T(8,128)(2,1)S(1)}, u32[]{:S(2)}, u32[]{:S(2)}) collective-permute-start(bf16[4,16,128]{2,1,0:T(8,128)(2,1)S(1)} %collective-permute-done.3), channel_id=1, source_target_pairs={{0,1},{1,2},{2,3},{3,4},{4,5},{5,6},{6,7},{7,8},{8,9},{9,10},{10,1... | collective-permute-start | bytes 49160 | tf_op jit(solution)/shard_map/ppermute | solution.py:52
  38.1 5.9 %collective-permute-start.5 = (bf16[4,16,128]{2,1,0:T(8,128)(2,1)S(1)}, bf16[4,16,128]{2,1,0:T(8,128)(2,1)S(1)}, u32[]{:S(2)}, u32[]{:S(2)}) collective-permute-start(bf16[4,16,128]{2,1,0:T(8,128)(2,1)S(1)} %collective-permute-done.4), channel_id=1, source_target_pairs={{0,1},{1,2},{2,3},{3,4},{4,5},{5,6},{6,7},{7,8},{8,9},{9,10},{10,1... | collective-permute-start | bytes 49160 | tf_op jit(solution)/shard_map/ppermute | solution.py:52
  43.9 5.9 %collective-permute-start.6 = (bf16[4,16,128]{2,1,0:T(8,128)(2,1)S(1)}, bf16[4,16,128]{2,1,0:T(8,128)(2,1)S(1)}, u32[]{:S(2)}, u32[]{:S(2)}) collective-permute-start(bf16[4,16,128]{2,1,0:T(8,128)(2,1)S(1)} %collective-permute-done.5), channel_id=1, source_target_pairs={{0,1},{1,2},{2,3},{3,4},{4,5},{5,6},{6,7},{7,8},{8,9},{9,10},{10,1... | collective-permute-start | bytes 49160 | tf_op jit(solution)/shard_map/ppermute | solution.py:52
  49.8 5.9 %collective-permute-start.7 = (bf16[4,16,128]{2,1,0:T(8,128)(2,1)S(1)}, bf16[4,16,128]{2,1,0:T(8,128)(2,1)S(1)}, u32[]{:S(2)}, u32[]{:S(2)}) collective-permute-start(bf16[4,16,128]{2,1,0:T(8,128)(2,1)S(1)} %collective-permute-done.6), channel_id=1, source_target_pairs={{0,1},{1,2},{2,3},{3,4},{4,5},{5,6},{6,7},{7,8},{8,9},{9,10},{10,1... | collective-permute-start | bytes 49160 | tf_op jit(solution)/shard_map/ppermute | solution.py:52
  55.6 5.9 %collective-permute-start.8 = (bf16[4,16,128]{2,1,0:T(8,128)(2,1)S(1)}, bf16[4,16,128]{2,1,0:T(8,128)(2,1)S(1)}, u32[]{:S(2)}, u32[]{:S(2)}) collective-permute-start(bf16[4,16,128]{2,1,0:T(8,128)(2,1)S(1)} %collective-permute-done.7), channel_id=1, source_target_pairs={{0,1},{1,2},{2,3},{3,4},{4,5},{5,6},{6,7},{7,8},{8,9},{9,10},{10,1... | collective-permute-start | bytes 49160 | tf_op jit(solution)/shard_map/ppermute | solution.py:52
  61.5 5.9 %collective-permute-start.9 = (bf16[4,16,128]{2,1,0:T(8,128)(2,1)S(1)}, bf16[4,16,128]{2,1,0:T(8,128)(2,1)S(1)}, u32[]{:S(2)}, u32[]{:S(2)}) collective-permute-start(bf16[4,16,128]{2,1,0:T(8,128)(2,1)S(1)} %collective-permute-done.8), channel_id=1, source_target_pairs={{0,1},{1,2},{2,3},{3,4},{4,5},{5,6},{6,7},{7,8},{8,9},{9,10},{10,1... | collective-permute-start | bytes 49160 | tf_op jit(solution)/shard_map/ppermute | solution.py:52
  67.4 5.9 %collective-permute-start.10 = (bf16[4,16,128]{2,1,0:T(8,128)(2,1)S(1)}, bf16[4,16,128]{2,1,0:T(8,128)(2,1)S(1)}, u32[]{:S(2)}, u32[]{:S(2)}) collective-permute-start(bf16[4,16,128]{2,1,0:T(8,128)(2,1)S(1)} %collective-permute-done.9), channel_id=1, source_target_pairs={{0,1},{1,2},{2,3},{3,4},{4,5},{5,6},{6,7},{7,8},{8,9},{9,10},{10,1... | collective-permute-start | bytes 49160 | tf_op jit(solution)/shard_map/ppermute | solution.py:52
  73.2 5.9 %collective-permute-start.11 = (bf16[4,16,128]{2,1,0:T(8,128)(2,1)S(1)}, bf16[4,16,128]{2,1,0:T(8,128)(2,1)S(1)}, u32[]{:S(2)}, u32[]{:S(2)}) collective-permute-start(bf16[4,16,128]{2,1,0:T(8,128)(2,1)S(1)} %collective-permute-done.10), channel_id=1, source_target_pairs={{0,1},{1,2},{2,3},{3,4},{4,5},{5,6},{6,7},{7,8},{8,9},{9,10},{10,1... | collective-permute-start | bytes 49160 | tf_op jit(solution)/shard_map/ppermute | solution.py:52
  79.1 5.9 %collective-permute-start.12 = (bf16[4,16,128]{2,1,0:T(8,128)(2,1)S(1)}, bf16[4,16,128]{2,1,0:T(8,128)(2,1)S(1)}, u32[]{:S(2)}, u32[]{:S(2)}) collective-permute-start(bf16[4,16,128]{2,1,0:T(8,128)(2,1)S(1)} %collective-permute-done.11), channel_id=1, source_target_pairs={{0,1},{1,2},{2,3},{3,4},{4,5},{5,6},{6,7},{7,8},{8,9},{9,10},{10,1... | collective-permute-start | bytes 49160 | tf_op jit(solution)/shard_map/ppermute | solution.py:52
  85.0 5.9 %collective-permute-start.13 = (bf16[4,16,128]{2,1,0:T(8,128)(2,1)S(1)}, bf16[4,16,128]{2,1,0:T(8,128)(2,1)S(1)}, u32[]{:S(2)}, u32[]{:S(2)}) collective-permute-start(bf16[4,16,128]{2,1,0:T(8,128)(2,1)S(1)} %collective-permute-done.12), channel_id=1, source_target_pairs={{0,1},{1,2},{2,3},{3,4},{4,5},{5,6},{6,7},{7,8},{8,9},{9,10},{10,1... | collective-permute-start | bytes 49160 | tf_op jit(solution)/shard_map/ppermute | solution.py:52
  90.8 5.9 %collective-permute-start.14 = (bf16[4,16,128]{2,1,0:T(8,128)(2,1)S(1)}, bf16[4,16,128]{2,1,0:T(8,128)(2,1)S(1)}, u32[]{:S(2)}, u32[]{:S(2)}) collective-permute-start(bf16[4,16,128]{2,1,0:T(8,128)(2,1)S(1)} %collective-permute-done.13), channel_id=1, source_target_pairs={{0,1},{1,2},{2,3},{3,4},{4,5},{5,6},{6,7},{7,8},{8,9},{9,10},{10,1... | collective-permute-start | bytes 49160 | tf_op jit(solution)/shard_map/ppermute | solution.py:52
  109.3 7.0 %all-to-all-start.5 = ((f32[2,1,512]{2,1,0:T(1,128)}), f32[2,1,512]{2,1,0:T(1,128)S(1)}, u32[]{:S(2)}, u32[]{:S(2)}) async-start(f32[2,1,512]{2,1,0:T(1,128)} %reshape.140), calls=%async_computation.5 | async-start | bytes 8192 | tf_op jit(solution)/shard_map/all_to_all | solution.py:119
  116.3 9.1 %all-to-all-start.3 = ((f32[2,1,512]{2,1,0:T(1,128)}), f32[2,1,512]{2,1,0:T(1,128)S(1)}, u32[]{:S(2)}, u32[]{:S(2)}) async-start(f32[2,1,512]{2,1,0:T(1,128)} %reshape.138), calls=%async_computation.3 | async-start | bytes 8192 | tf_op jit(solution)/shard_map/all_to_all | solution.py:106
  125.3 10.1 %all-to-all-start.6 = ((f32[32,1,32]{2,1,0:T(1,128)}), f32[32,1,32]{2,1,0:T(1,128)S(1)}, u32[]{:S(2)}, u32[]{:S(2)}) async-start(f32[32,1,32]{2,1,0:T(1,128)} %copy.100), calls=%async_computation.6 | async-start | bytes 32768 | tf_op jit(solution)/shard_map/all_to_all | solution.py:118
  135.4 12.4 %all-to-all-start.1 = ((f32[64,1,16,128]{3,2,1,0:T(8,128)}), f32[64,1,16,128]{3,2,1,0:T(8,128)S(1)}, u32[]{:S(2)}, u32[]{:S(2)}) async-start(f32[64,1,16,128]{3,2,1,0:T(8,128)} %bitcast.14), calls=%async_computation.1 | async-start | bytes 1048576 | tf_op jit(solution)/shard_map/all_to_all | solution.py:93
  147.9 12.3 %all-to-all-start.4 = ((f32[32,1,32]{2,1,0:T(1,128)}), f32[32,1,32]{2,1,0:T(1,128)S(1)}, u32[]{:S(2)}, u32[]{:S(2)}) async-start(f32[32,1,32]{2,1,0:T(1,128)} %copy.93), calls=%async_computation.4 | async-start | bytes 32768 | tf_op jit(solution)/shard_map/all_to_all | solution.py:105
  160.2 17.8 %all-to-all-start.2 = ((f32[32,1,32,128]{3,2,1,0:T(8,128)}), f32[32,1,32,128]{3,2,1,0:T(8,128)S(1)}, u32[]{:S(2)}, u32[]{:S(2)}) async-start(f32[32,1,32,128]{3,2,1,0:T(8,128)} %bitcast.18), calls=%async_computation.2 | async-start | bytes 1048576 | tf_op jit(solution)/shard_map/all_to_all | solution.py:92
